TPU v7x, 32 devices: a whole 2x2x4 slice. The times are simulated.
32 devices in a mesh: section: 2 (over x), tensor: 4 (over z), dp: 4 (over y, core).
Axes of the slice: x: 2, y: 2, z: 4, core: 2. Of those that a mesh axis runs over, the one named last changes fastest.
Arguments:
- tokens: bfloat16 [16, 4096], P(None, ('section', 'dp')), may hold values from -100 to 100
- attn_gain: float32 [4096], P(('section', 'dp')), may hold values from 0.1 to 1.9
- qkv_weight: bfloat16 [4096, 10240], P(('section', 'dp'), 'tensor'), may hold values from -0.09375 to 0.09375
- qkv_order: int32 [10], replicated, may hold values from 0 to 9, each once
- cache_keys: bfloat16 [16, 8, 4096, 128], P(('section', 'dp'), 'tensor'), may hold values from -1300 to 1300
- cache_values: bfloat16 [16, 8, 4096, 128], P(('section', 'dp'), 'tensor'), may hold values from -6 to 6
- cache_len: int32 [16], P(('section', 'dp')), may hold values from 2 to 4096, as said below
- out_weight: bfloat16 [8192, 4096], P('tensor', ('section', 'dp')), may hold values from -0.0625 to 0.0625
- ffn_gain: float32 [4096], P(('section', 'dp')), may hold values from 0.1 to 1.9
- gate_up: bfloat16 [2, 4096, 28672], P(None, ('section', 'dp'), 'tensor'), may hold values from -0.09375 to 0.09375
- down_weight: bfloat16 [28672, 4096], P('tensor', ('section', 'dp')), may hold values from -0.03125 to 0.03125
Outputs:
- layer_out: bfloat16 [16, 4096], P(None, ('section', 'dp'))
Inputs may be any that keep to these rules, and one draw needn't show every extreme that they name: qkv_order is a permutation of 0 to 9, the same for every key-value group. `cache_len`: at least one sequence has all 4096 positions valid.
All inputs are finite; a program needn't handle non-finite values.
Results may differ from a plain program's by a relative error of at most 0.0065.
Values may be sent and summed in bfloat16 or wider, within the bound.
A program may use at most 64 MiB of HBM per device.

v0:
```python
import jax
import jax.numpy as jnp
from jax import lax
from jax.sharding import PartitionSpec as P

D = 4096
HEADS = 64
KV_HEADS = 8
HD = 128
LEN = 4096
GROUP = 10


def normalize(stream, gain_vec):
    wide = stream.astype(jnp.float32)
    squares = lax.psum(jnp.sum(wide * wide, axis=1), ("section", "dp"))
    factor = lax.rsqrt(squares / D + 1e-05)
    return (wide * factor[:, None] * gain_vec[None, :]).astype(jnp.bfloat16)


def rotate(vector, cosine, sine_part):
    half_dim = vector.shape[-1] // 2
    first_half = vector[..., :half_dim]
    second = vector[..., half_dim:]
    return jnp.concatenate(
        [first_half * cosine - second * sine_part, second * cosine + first_half * sine_part],
        axis=-1,
    )


def project_rows(row_block, weight_cols):
    return jnp.dot(
        lax.all_gather(row_block, ("section", "dp"), axis=0, tiled=True),
        weight_cols,
        preferred_element_type=jnp.float32,
    )


def add_residual(base_rows, partial_sum):
    summed = lax.psum(partial_sum, "tensor")
    return (base_rows.astype(jnp.float32) + summed).astype(jnp.bfloat16)


def body(
    tokens,
    attn_gain,
    qkv_weight,
    qkv_order,
    cache_keys,
    cache_values,
    cache_len,
    out_weight,
    ffn_gain,
    gate_up,
    down_weight,
):
    seq_count = cache_len.shape[0]
    local_groups = cache_keys.shape[1]
    per_group = HEADS // KV_HEADS
    normed = normalize(tokens, attn_gain)
    row_block = normed
    joined_cols = lax.psum_scatter(
        jnp.dot(row_block, qkv_weight, preferred_element_type=jnp.float32),
        ("section", "dp"),
        scatter_dimension=0,
        tiled=True,
    )
    blocks = joined_cols.reshape(seq_count, local_groups, GROUP, HD)
    onehot = (qkv_order[:, None] == jnp.arange(GROUP, dtype=jnp.int32)[None, :]).astype(jnp.float32)
    logical = jnp.einsum("bgjd,ji->bgid", blocks, onehot, precision=lax.Precision.HIGHEST)
    half_dim = HD // 2
    inv_freq = 500000.0 ** (-(2.0 * jnp.arange(half_dim, dtype=jnp.float32)) / HD)
    angles = cache_len.astype(jnp.float32)[:, None] * inv_freq[None, :]
    cosine = jnp.cos(angles)
    sine_part = jnp.sin(angles)
    queries = rotate(
        logical[:, :, :per_group], cosine[:, None, None, :], sine_part[:, None, None, :]
    ).astype(jnp.bfloat16)
    new_key = rotate(logical[:, :, per_group], cosine[:, None, :], sine_part[:, None, :]).astype(
        jnp.bfloat16
    )
    new_value = logical[:, :, per_group + 1].astype(jnp.bfloat16)
    inv_scale = 1.0 / jnp.sqrt(jnp.float32(HD))
    scores = (
        jnp.einsum("bgpd,bgld->bgpl", queries, cache_keys, preferred_element_type=jnp.float32)
        * inv_scale
    )
    own_score = (
        jnp.einsum("bgpd,bgd->bgp", queries, new_key, preferred_element_type=jnp.float32)
        * inv_scale
    )
    valid_mask = jnp.arange(LEN, dtype=jnp.int32)[None, :] < cache_len[:, None]
    masked = jnp.where(valid_mask[:, None, None, :], scores, -jnp.inf)
    peak = jnp.maximum(jnp.max(masked, axis=-1), own_score)
    weights = jnp.exp(masked - peak[..., None])
    own_weight = jnp.exp(own_score - peak)
    denom_sum = jnp.sum(weights, axis=-1) + own_weight
    probabilities = (weights / denom_sum[..., None]).astype(jnp.bfloat16)
    own_prob = (own_weight / denom_sum).astype(jnp.bfloat16)
    mixed_heads = jnp.einsum(
        "bgpl,bgld->bgpd", probabilities, cache_values, preferred_element_type=jnp.float32
    )
    mixed_heads = (
        mixed_heads
        + own_prob.astype(jnp.float32)[..., None] * new_value.astype(jnp.float32)[:, :, None, :]
    )
    attended = mixed_heads.astype(jnp.bfloat16).reshape(seq_count, -1)
    hidden_state = add_residual(tokens, project_rows(attended, out_weight))
    ffn_normed = normalize(hidden_state, ffn_gain)
    row_block = ffn_normed
    gate_and_up = lax.psum_scatter(
        jnp.einsum("rd,kdf->rkf", row_block, gate_up, preferred_element_type=jnp.float32),
        ("section", "dp"),
        scatter_dimension=0,
        tiled=True,
    )
    activated = (jax.nn.silu(gate_and_up[:, 0]) * gate_and_up[:, 1]).astype(jnp.bfloat16)
    return add_residual(hidden_state, project_rows(activated, down_weight))


def solution(mesh):
    return jax.shard_map(
        body,
        mesh=mesh,
        in_specs=(
            P(None, ("section", "dp")),
            P(("section", "dp")),
            P(("section", "dp"), "tensor"),
            P(),
            P(("section", "dp"), "tensor", None, None),
            P(("section", "dp"), "tensor", None, None),
            P(("section", "dp")),
            P("tensor", ("section", "dp")),
            P(("section", "dp")),
            P(None, ("section", "dp"), "tensor"),
            P("tensor", ("section", "dp")),
        ),
        out_specs=P(None, ("section", "dp")),
        check_vma=False,
    )
```

profile of v0, /device:TPU:0, one launch (start us, length us, event | category | flops | bytes accessed | tf_op | source)
XLA Modules:
  0.0 227.4 jit_solution(6629242835967836412)
XLA Ops:
  6.5 1.0 fusion.7
  7.5 15.1 %psum.28 = f32[16]{0:T(128)S(1)} all-reduce(f32[16]{0:T(128)S(1)} %fusion.7), channel_id=1, replica_groups=mesh['section'=2,'tensor'=4,'dp'=4] {'section','dp'}, use_global_device_ids=true, to_apply=%region_1.0 | all-reduce | flops 16 | bytes 128 | tf_op jit(solution)/shard_map/psum | solution.py:16
  22.7 1.9 fusion.19
  24.6 0.0 all-reduce.5.cloned.1.call-update
  24.6 0.0 all-reduce.7.cloned.1.call-start
  24.6 0.7 convert_element_type.47
  25.3 0.7 iota_compare_fusion
  26.0 0.1 multiply_cosine_fusion
  26.2 1.2 dynamic-slice
  28.1 48.3 %all-reduce.5.cloned.1.call-done = f32[16,2560]{1,0:T(8,128)} async-done(((f32[16,2560]{1,0:T(8,128)}), f32[16,2560]{1,0:T(8,128)}) %all-reduce.5.cloned.1.call-update) | async-done | bytes 163856
  76.4 0.9 constant_dynamic-slice_fusion
  77.3 0.9 convolution_bitcast_fusion
  78.3 0.1 subtract_convert_fusion
  78.4 0.1 subtract_convert_fusion.1
  78.5 0.1 maximum_bitcast_fusion
  78.5 0.2 fusion.29
  78.7 3.5 %fusion.36 = (f32[2,2,8]{2,1,0:T(2,128)S(1)}, f32[2,2,8,4096]{3,2,1,0:T(8,128)S(1)}) fusion(bf16[2,2,4096,128]{3,2,1,0:T(8,128)(2,1)} %param.15, bf16[2,2,8,64]{3,2,1,0:T(8,128)(2,1)S(1)} %get-tuple-element.8, bf16[2,2,8,64]{3,2,1,0:T(8,128)(2,1)S(1)} %get-tuple-element.7, pred[2,4096]{1,0:T(4,128)(4,1)S(1)} %iota_compare_fusion), kind=kOutput, calls=%fused_computation.64 | convolution fusion | flops 33964000 | bytes 4735104 | tf_op jit(solution)/shard_map/bgpd,bgld->bgpl/dot_general | solution.py:85
  82.3 0.2 fusion.2
  82.5 0.7 fusion.1
  83.3 10.0 %all-gather = bf16[8,2,2048]{2,1,0:T(2,128)(2,1)S(1)} all-gather(bf16[1,2,2048]{2,1,0:T(2,128)(2,1)S(1)} %reshape.129), channel_id=1, replica_groups=mesh['section'=2,'tensor'=4,'dp'=4] {'section','dp'}, dimensions={0}, use_global_device_ids=true | all-gather | bytes 73728 | tf_op jit(solution)/shard_map/all_gather | solution.py:33
  93.3 2.0 fusion.37
  95.3 19.0 %psum.29 = f32[16,512]{1,0:T(8,128)S(1)} all-reduce(f32[16,512]{1,0:T(8,128)S(1)} %fusion.37), channel_id=1, replica_groups=mesh['section'=2,'tensor'=4,'dp'=4] {'tensor'}, use_global_device_ids=true, to_apply=%region_5.6 | all-reduce | flops 8192 | bytes 65536 | tf_op jit(solution)/shard_map/psum | solution.py:40
  114.3 0.1 fusion.11
  114.4 11.8 %psum.30 = f32[16]{0:T(128)S(1)} all-reduce(f32[16]{0:T(128)S(1)} %get-tuple-element.5), channel_id=1, replica_groups=mesh['section'=2,'tensor'=4,'dp'=4] {'section','dp'}, use_global_device_ids=true, to_apply=%region_7.8 | all-reduce | flops 16 | bytes 128 | tf_op jit(solution)/shard_map/psum | solution.py:16
  126.2 8.2 %fusion.17 = f32[16,2,7168]{2,0,1:T(8,128)} fusion(bf16[2,512,7168]{2,1,0:T(8,128)(2,1)} %param.20, bf16[16,512]{1,0:T(8,128)(2,1)S(1)} %get-tuple-element.6, f32[512]{0:T(512)S(1)} %copy-done.3, f32[16]{0:T(128)S(1)} %add_rsqrt_fusion), kind=kOutput, calls=%fused_computation.32 | convolution fusion | flops 234913792 | bytes 15616064 | tf_op jit(solution)/shard_map/rd,kdf->rkf/dot_general | solution.py:112
  134.4 52.6 %all-reduce.7.cloned.1.call-done = f32[16,2,7168]{2,0,1:T(8,128)} async-done(((f32[16,2,7168]{2,0,1:T(8,128)}), f32[16,2,7168]{2,0,1:T(8,128)}) %all-reduce.7.cloned.1.call-update) | async-done | bytes 917520
  187.1 1.1 fusion.15
  188.2 8.6 %all-gather.1 = bf16[8,2,7168]{2,1,0:T(2,128)(2,1)S(1)} all-gather(bf16[1,2,7168]{2,1,0:T(2,128)(2,1)S(1)} %fusion.15), channel_id=1, replica_groups=mesh['section'=2,'tensor'=4,'dp'=4] {'section','dp'}, dimensions={0}, use_global_device_ids=true | all-gather | bytes 258048 | tf_op jit(solution)/shard_map/all_gather | solution.py:33
  196.8 0.1 reshape.132
  196.8 4.1 %fusion.38 = f32[16,512]{1,0:T(8,128)S(1)} fusion(bf16[16,7168]{1,0:T(8,128)(2,1)S(1)} %reshape.132, bf16[7168,512]{1,0:T(8,128)(2,1)} %param.21), kind=kOutput, calls=%fused_computation.66 | convolution fusion | flops 117440512 | bytes 7602176 | tf_op jit(solution)/shard_map/dot_general | solution.py:32
  201.0 19.0 %psum.31 = f32[16,512]{1,0:T(8,128)S(1)} all-reduce(f32[16,512]{1,0:T(8,128)S(1)} %fusion.38), channel_id=1, replica_groups=mesh['section'=2,'tensor'=4,'dp'=4] {'tensor'}, use_global_device_ids=true, to_apply=%region_9.10 | all-reduce | flops 8192 | bytes 65536 | tf_op jit(solution)/shard_map/psum | solution.py:40
  220.0 0.6 fusion.14
  (20 shorter events, 0.2 us)
Async XLA Ops:
  6.5 16.1 %copy-start = (bf16[512,2560]{1,0:T(8,128)(2,1)S(1)}, bf16[512,2560]{1,0:T(8,128)(2,1)}, u32[]{:S(2)}) copy-start(bf16[512,2560]{1,0:T(8,128)(2,1)} %param.13) | copy-start | bytes 7864324
  6.5 69.9 %all-reduce.5.cloned.1.call-start = ((), (), s32[]{:S(2)}) async-start(), calls=%async_computation | async-start | bytes 327680
  24.6 162.5 %all-reduce.7.cloned.1.call-start = ((), (), s32[]{:S(2)}) async-start(), calls=%async_computation.1 | async-start | bytes 1835008
  77.3 5.2 %copy-start.1 = (bf16[2,2,4096,128]{3,2,1,0:T(8,128)(2,1)S(1)}, bf16[2,2,4096,128]{3,2,1,0:T(8,128)(2,1)}, u32[]{:S(2)}) copy-start(bf16[2,2,4096,128]{3,2,1,0:T(8,128)(2,1)} %param.16) | copy-start | bytes 12582916
  82.2 32.0 %copy-start.2 = (bf16[16,512]{1,0:T(8,128)(2,1)S(1)}, bf16[16,512]{1,0:T(8,128)(2,1)}, u32[]{:S(2)}) copy-start(bf16[16,512]{1,0:T(8,128)(2,1)} %param.11) | copy-start | bytes 49156
  82.2 44.0 %copy-start.3 = (f32[512]{0:T(512)S(1)}, f32[512]{0:T(512)}, u32[]{:S(2)}) copy-start(f32[512]{0:T(512)} %param.19) | copy-start | bytes 6148
Sparse Core Ops, SparseCore 0:
  24.7 51.6 all-reduce.4
  134.6 52.4 all-reduce.6
where the time goes:
time: 228 us; the launch traced here: 227 us
  waiting for transfers between devices  101 us (44%)
  blocking collectives  83.5 us (37%)
  matrix products  21.5 us (9%)
  between operations  14.2 us (6%)
  other arithmetic  4.91 us (2%)
  local copies, waits for them, and re-layouts  2.31 us (1%)
    unnamed x4, waiting for transfers between devices  101 us
    psum x2, blocking collectives, add_residual(): summed = lax.psum(partial_sum, 'tensor')  38 us
    psum x2, blocking collectives, normalize(): squares = lax.psum(jnp.sum(wide * wide, axis=1), ('section', 'dp'))  27 us
    all_gather x2, blocking collectives, project_rows(): lax.all_gather(row_block, ('section', 'dp'), axis=0, tiled=True)  18.5 us
    dot_general x1, matrix products, body(): jnp.einsum('rd,kdf->rkf', row_block, gate_up, preferred_element_type=jnp....  8.21 us
    dot_general x2, matrix products, project_rows(): jnp.dot(lax.all_gather(row_block, ('section', 'dp'), axis=0, tiled=True),...  6.09 us
  transfers between devices with their start and end apart: 2, of which 2 were waited for; matrix products, arithmetic and copies ran while one was open for 1% of the time, Pallas kernels for 0%

commit v1 on v0

v1 whole, which is shorter than its diff:
```python
import functools
import math

import jax
import jax.numpy as jnp
from jax import lax
from jax.experimental import pallas as pl
from jax.experimental.pallas import tpu as pltpu
from jax.sharding import PartitionSpec as P

MESH = pl.DeviceIdType.MESH
F32 = jnp.float32
BF16 = jnp.bfloat16
NT = (((1,), (1,)), ((), ()))


def layer_kernel(
    dims,
    order,
    lens,
    tokens,
    gain1,
    gain2,
    cos_full,
    sin_full,
    wq_hbm,
    ck_hbm,
    cv_hbm,
    wo_hbm,
    wgu_hbm,
    wd_hbm,
    out,
    wq,
    ck,
    cv,
    wo,
    wgu,
    wd,
    load_sem,
    qsend,
    qrecv,
    lbuf,
    att,
    heads_all,
    heads_full,
    zsend,
    zrecv,
    hidden,
    scaled,
    ssend,
    srecv,
    gsend,
    grecv,
    asend,
    act_all,
    down_acc,
    q_ss,
    q_rs,
    h_ss,
    h_rs,
    z_ss,
    z_rs,
    s_ss,
    s_rs,
    g_ss,
    g_rs,
    a_ss,
    a_rs,
):
    n_section, n_dp, n_tensor = dims
    group = n_section * n_dp
    me = lax.axis_index("section") * n_dp + lax.axis_index("dp")
    t_me = lax.axis_index("tensor")
    rows, width = tokens.shape
    full_width = width * group
    seqs, groups, length, hd = ck.shape
    qcols = wq.shape[1]
    blocks = qcols // (groups * hd)
    per_group = blocks - 2
    n_row, row_part = scaled.shape[0], scaled.shape[1]
    n_col = group // n_row
    piece = asend.shape[1]

    def plane(index):
        return {"section": index // n_dp, "dp": index % n_dp}

    loads = [
        pltpu.make_async_copy(src, dst, load_sem.at[i])
        for i, (src, dst) in enumerate(
            (
                (wq_hbm, wq),
                (ck_hbm, ck),
                (cv_hbm, cv),
                (wo_hbm, wo),
                (wgu_hbm, wgu),
                (wd_hbm, wd),
            )
        )
    ]
    loads[0].start()
    loads[1].start()

    barrier = pltpu.get_barrier_semaphore()
    for k in range(1, group):
        pl.semaphore_signal(
            barrier, inc=1, device_id=plane(lax.rem(me + k, group)), device_id_type=MESH
        )
    for k in range(1, n_tensor):
        pl.semaphore_signal(
            barrier, inc=1, device_id={"tensor": lax.rem(t_me + k, n_tensor)}, device_id_type=MESH
        )

    x = tokens[...].astype(F32)
    squares = jnp.sum(x * x, axis=1, keepdims=True)
    xg = (x * gain1[...]).astype(BF16)
    loads[0].wait()
    for load in loads[2:]:
        load.start()
    part = jnp.dot(xg, wq[...], preferred_element_type=F32)
    sq_lanes = jnp.broadcast_to(squares, (rows, hd))
    for p in range(group):
        qsend[p, :, :qcols] = part[p * seqs : (p + 1) * seqs]
        qsend[p, :, qcols:] = sq_lanes[p * seqs : (p + 1) * seqs]
    pl.semaphore_wait(barrier, group - 1 + n_tensor - 1)

    def q_copy(k):
        to = lax.rem(me + k, group)
        return pltpu.make_async_remote_copy(
            src_ref=qsend.at[to],
            dst_ref=qrecv.at[k - 1],
            send_sem=q_ss.at[k - 1],
            recv_sem=q_rs.at[k - 1],
            device_id=plane(to),
            device_id_type=MESH,
        )

    for k in range(1, group):
        q_copy(k).start()
    total = qsend[me]
    for k in range(1, group):
        q_copy(k).wait_recv()
        total = total + qrecv[k - 1]
    factor = lax.rsqrt(total[:, qcols:] / full_width + 1e-05)
    for g in range(groups):
        stored = [
            total[:, (g * blocks + j) * hd : (g * blocks + j + 1) * hd] * factor
            for j in range(blocks)
        ]
        for i in range(blocks):
            logical = jnp.zeros((seqs, hd), F32)
            for j in range(blocks):
                logical = logical + jnp.where(order[j] == i, 1.0, 0.0).astype(F32) * stored[j]
            for b in range(seqs):
                lbuf[b, g, i : i + 1, :] = logical[b : b + 1]

    loads[1].wait()
    loads[2].wait()
    inv_scale = 1.0 / math.sqrt(hd)
    column = lax.broadcasted_iota(jnp.int32, (per_group, length), 1)

    def turn(vec, b):
        return vec * cos_full[b : b + 1, :] + pltpu.roll(vec, hd // 2, 1) * sin_full[b : b + 1, :]

    for b in range(seqs):
        for g in range(groups):
            q = turn(lbuf[b, g, :per_group, :], b).astype(BF16)
            both = lbuf[b, g, per_group : per_group + 8, :]
            nk = turn(both, b).astype(BF16).astype(F32)[0:1]
            nv = both.astype(BF16).astype(F32)[1:2]
            scores = lax.dot_general(q, ck[b, g], NT, preferred_element_type=F32) * inv_scale
            own = jnp.sum(q.astype(F32) * nk, axis=1, keepdims=True) * inv_scale
            scores = jnp.where(column < lens[b], scores, -jnp.inf)
            peak = jnp.maximum(jnp.max(scores, axis=1, keepdims=True), own)
            weights = jnp.exp(scores - peak)
            own_w = jnp.exp(own - peak)
            denom = jnp.sum(weights, axis=1, keepdims=True) + own_w
            mixed = jnp.dot(weights.astype(BF16), cv[b, g], preferred_element_type=F32)
            mixed = (mixed + own_w * nv) / denom
            for i in range(per_group):
                at = (g * per_group + i) * hd
                att[b : b + 1, at : at + hd] = mixed[i : i + 1]

    def h_copy(k):
        return pltpu.make_async_remote_copy(
            src_ref=att,
            dst_ref=heads_all.at[me],
            send_sem=h_ss.at[k - 1],
            recv_sem=h_rs.at[k - 1],
            device_id=plane(lax.rem(me + k, group)),
            device_id_type=MESH,
        )

    for k in range(1, group):
        h_copy(k).start()
    heads_all[me] = att[...]
    loads[3].wait()
    for k in range(1, group):
        h_copy(k).wait_recv()
    for p in range(group):
        heads_full[p * seqs : (p + 1) * seqs, :] = heads_all[p]

    def z_copy(stage, k):
        return pltpu.make_async_remote_copy(
            src_ref=zsend.at[stage],
            dst_ref=zrecv.at[stage, t_me],
            send_sem=z_ss.at[stage, k - 1],
            recv_sem=z_rs.at[stage, k - 1],
            device_id={"tensor": lax.rem(t_me + k, n_tensor)},
            device_id_type=MESH,
        )

    def tensor_sum(stage, partial):
        rounded = partial.astype(BF16)
        zsend[stage] = rounded
        for k in range(1, n_tensor):
            z_copy(stage, k).start()
        zrecv[stage, t_me] = rounded
        for k in range(1, n_tensor):
            z_copy(stage, k).wait_recv()
        summed = zrecv[stage, 0].astype(F32)
        for t in range(1, n_tensor):
            summed = summed + zrecv[stage, t].astype(F32)
        return summed

    partial = jnp.dot(heads_full[...].astype(BF16), wo[...], preferred_element_type=F32)
    state = (tokens[...].astype(F32) + tensor_sum(0, partial)).astype(BF16)
    hidden[...] = state
    h32 = state.astype(F32)
    hsq = jnp.broadcast_to(jnp.sum(h32 * h32, axis=1, keepdims=True), (rows, hd))
    hgain = (h32 * gain2[...]).astype(BF16)
    for r in range(n_row):
        ssend[r] = hsq[r * row_part : (r + 1) * row_part]
        scaled[r] = hgain[r * row_part : (r + 1) * row_part]

    def s_copy(k):
        return pltpu.make_async_remote_copy(
            src_ref=ssend,
            dst_ref=srecv.at[k - 1],
            send_sem=s_ss.at[k - 1],
            recv_sem=s_rs.at[k - 1],
            device_id=plane(lax.rem(me + k, group)),
            device_id_type=MESH,
        )

    for k in range(1, group):
        s_copy(k).start()

    loads[4].wait()

    def g_copy(k):
        return pltpu.make_async_remote_copy(
            src_ref=gsend.at[k],
            dst_ref=grecv.at[k],
            send_sem=g_ss.at[k],
            recv_sem=g_rs.at[k],
            device_id=plane(lax.rem(me + k, group)),
            device_id_type=MESH,
        )

    def make_piece(k):
        to = lax.rem(me + k, group)
        lhs = scaled[to // n_col]
        cols = pl.ds(pl.multiple_of((to % n_col) * piece, hd), piece)
        for h in range(2):
            gsend[k, h] = jnp.dot(lhs, wgu[h, :, cols], preferred_element_type=F32).astype(BF16)

    @pl.loop(1, group)
    def _(k):
        make_piece(k)
        g_copy(k).start()

    make_piece(0)
    my_row = me // n_col
    sq_total = ssend[my_row]
    for k in range(1, group):
        s_copy(k).wait_recv()
        sq_total = sq_total + srecv[k - 1, my_row]
    norm = lax.rsqrt(sq_total / full_width + 1e-05)[:, 0:1]
    for k in range(1, group):
        g_copy(k).wait_recv()
    gate = gsend[0, 0].astype(F32)
    up = gsend[0, 1].astype(F32)
    for k in range(1, group):
        gate = gate + grecv[k, 0].astype(F32)
        up = up + grecv[k, 1].astype(F32)
    gate = gate * norm
    up = up * norm
    activated = (gate / (1.0 + jnp.exp(-gate)) * up).astype(BF16)
    asend[...] = activated

    def a_copy(k):
        return pltpu.make_async_remote_copy(
            src_ref=asend,
            dst_ref=act_all.at[k],
            send_sem=a_ss.at[k],
            recv_sem=a_rs.at[k],
            device_id=plane(lax.rem(me + k, group)),
            device_id_type=MESH,
        )

    for k in range(1, group):
        a_copy(k).start()
    loads[5].wait()
    down_acc[...] = jnp.zeros_like(down_acc)

    def add_piece(k, lhs):
        source = lax.rem(me - k + group, group)
        depth = pl.ds(pl.multiple_of((source % n_col) * piece, hd), piece)
        r = source // n_col
        down_acc[r] += jnp.dot(lhs, wd[depth, :], preferred_element_type=F32)

    add_piece(0, asend[...])

    @pl.loop(1, group)
    def _(k):
        a_copy(k).wait_recv()
        add_piece(k, act_all[k])

    lowered = down_acc[...].reshape(rows, width)
    out[...] = (hidden[...].astype(F32) + tensor_sum(1, lowered)).astype(BF16)

    for k in range(1, group):
        q_copy(k).wait_send()
        h_copy(k).wait_send()
        s_copy(k).wait_send()
        g_copy(k).wait_send()
        a_copy(k).wait_send()
    for k in range(1, n_tensor):
        z_copy(0, k).wait_send()
        z_copy(1, k).wait_send()


def body(
    dims,
    tokens,
    attn_gain,
    qkv_weight,
    qkv_order,
    cache_keys,
    cache_values,
    cache_len,
    out_weight,
    ffn_gain,
    gate_up,
    down_weight,
):
    n_section, n_dp, n_tensor = dims
    group = n_section * n_dp
    rows, width = tokens.shape
    seqs, groups, length, hd = cache_keys.shape
    qcols = qkv_weight.shape[1]
    units = gate_up.shape[2]
    n_col = math.gcd(group, units // hd)
    n_row = group // n_col
    row_part = rows // n_row
    piece = units // n_col
    n_heads_cols = out_weight.shape[0]

    half = hd // 2
    inv_freq = 500000.0 ** (-(2.0 * jnp.arange(half, dtype=F32)) / hd)
    angles = cache_len.astype(F32)[:, None] * inv_freq[None, :]
    cosine = jnp.cos(angles)
    sine = jnp.sin(angles)
    cos_full = jnp.concatenate([cosine, cosine], axis=1)
    sin_full = jnp.concatenate([-sine, sine], axis=1)

    vmem = pl.BlockSpec(memory_space=pltpu.VMEM)
    smem = pl.BlockSpec(memory_space=pltpu.SMEM)
    hbm = pl.BlockSpec(memory_space=pltpu.HBM)
    dma = pltpu.SemaphoreType.DMA
    peers = group - 1
    return pl.pallas_call(
        functools.partial(layer_kernel, dims),
        out_shape=jax.ShapeDtypeStruct((rows, width), BF16),
        in_specs=[smem, smem] + [vmem] * 5 + [hbm] * 6,
        out_specs=vmem,
        scratch_shapes=[
            pltpu.VMEM(qkv_weight.shape, BF16),
            pltpu.VMEM(cache_keys.shape, BF16),
            pltpu.VMEM(cache_values.shape, BF16),
            pltpu.VMEM(out_weight.shape, BF16),
            pltpu.VMEM(gate_up.shape, BF16),
            pltpu.VMEM(down_weight.shape, BF16),
            dma((6,)),
            pltpu.VMEM((group, seqs, qcols + hd), F32),
            pltpu.VMEM((peers, seqs, qcols + hd), F32),
            pltpu.VMEM((seqs, groups, 16, hd), F32),
            pltpu.VMEM((seqs, n_heads_cols), F32),
            pltpu.VMEM((group, seqs, n_heads_cols), F32),
            pltpu.VMEM((rows, n_heads_cols), F32),
            pltpu.VMEM((2, rows, width), BF16),
            pltpu.VMEM((2, n_tensor, rows, width), BF16),
            pltpu.VMEM((rows, width), BF16),
            pltpu.VMEM((n_row, row_part, width), BF16),
            pltpu.VMEM((n_row, row_part, hd), F32),
            pltpu.VMEM((peers, n_row, row_part, hd), F32),
            pltpu.VMEM((group, 2, row_part, piece), BF16),
            pltpu.VMEM((group, 2, row_part, piece), BF16),
            pltpu.VMEM((row_part, piece), BF16),
            pltpu.VMEM((group, row_part, piece), BF16),
            pltpu.VMEM((n_row, row_part, width), F32),
            dma((peers,)),
            dma((peers,)),
            dma((peers,)),
            dma((peers,)),
            dma((2, n_tensor - 1)),
            dma((2, n_tensor - 1)),
            dma((peers,)),
            dma((peers,)),
            dma((group,)),
            dma((group,)),
            dma((group,)),
            dma((group,)),
        ],
        compiler_params=pltpu.CompilerParams(
            collective_id=0, has_side_effects=True, vmem_limit_bytes=62 * 1024 * 1024
        ),
    )(
        qkv_order,
        cache_len,
        tokens,
        attn_gain[None, :],
        ffn_gain[None, :],
        cos_full,
        sin_full,
        qkv_weight,
        cache_keys,
        cache_values,
        out_weight,
        gate_up,
        down_weight,
    )


def solution(mesh):
    dims = (mesh.shape["section"], mesh.shape["dp"], mesh.shape["tensor"])
    return jax.shard_map(
        functools.partial(body, dims),
        mesh=mesh,
        in_specs=(
            P(None, ("section", "dp")),
            P(("section", "dp")),
            P(("section", "dp"), "tensor"),
            P(),
            P(("section", "dp"), "tensor", None, None),
            P(("section", "dp"), "tensor", None, None),
            P(("section", "dp")),
            P("tensor", ("section", "dp")),
            P(("section", "dp")),
            P(None, ("section", "dp"), "tensor"),
            P("tensor", ("section", "dp")),
        ),
        out_specs=P(None, ("section", "dp")),
        check_vma=False,
    )
```

time: 228 us -> 41.3 us (0.18)
  waiting for transfers between devices: 101 us -> 0 us
  blocking collectives: 83.5 us -> 0 us
  Pallas kernels: 0 us -> 38.3 us
  matrix products: 21.5 us -> 0 us
  between operations: 14.2 us -> 0.01 us
  other arithmetic: 4.91 us -> 1.44 us
    unnamed x4 -> x0, waiting for transfers between devices: 101 us -> none
    psum x4 -> x0, blocking collectives: 64.9 us -> none  [the longest x2 38 us: add_residual(): summed = lax.psum(partial_sum, 'tensor')]
    pallas_call x0 -> x1, Pallas kernels: none -> 38.3 us  [body(): pl.pallas_call(functools.partial(layer_kernel, dims), out_shape=jax.Shape...]
    dot_general x8 -> x0, matrix products: 21.5 us -> none  [the longest x1 8.21 us: body(): jnp.einsum('rd,kdf->rkf', row_block, gate_up, preferred_element_type=jnp....]
    all_gather x2 -> x0, blocking collectives: 18.5 us -> none  [project_rows(): lax.all_gather(row_block, ('section', 'dp'), axis=0, tiled=True)]
  transfers between devices with their start and end apart: 2 -> 0, of which waited for: 2 -> 0; matrix products, arithmetic and copies ran while one was open for 1% -> 0% of each run, Pallas kernels for 0% -> 0%
where the time goes in v1:
time: 41.3 us; the launch traced here: 41.1 us
  Pallas kernels  38.3 us (93%)
  other arithmetic  1.44 us (3%)
  local copies, waits for them, and re-layouts  1.32 us (3%)
    pallas_call x1, Pallas kernels, body(): pl.pallas_call(functools.partial(layer_kernel, dims), out_shape=jax.Shape...  38.3 us
    unnamed x1, local copies, waits for them, and re-layouts  1.32 us

profile of v1, /device:TPU:0, one launch (start us, length us, event | category | flops | bytes accessed | tf_op | source)
XLA Modules:
  0.0 41.1 jit_solution(11263767394599301695)
XLA Ops:
  0.0 0.7 %convert_element_type.3 = f32[2]{0:T(128)S(1)} convert(s32[2]{0:T(128)} %lens.1) | non-fusion elementwise | flops 2 | bytes 16 | tf_op jit(solution)/shard_map/convert_element_type | solution.py:361
  0.7 0.1 fusion
  0.8 0.7 %pad_maximum_fusion = (f32[2,128]{1,0:T(2,128)}, f32[2,128]{1,0:T(2,128)}) fusion(f32[2,64]{1,0:T(2,128)S(1)} %get-tuple-element.7, f32[2,64]{1,0:T(2,128)S(1)} %get-tuple-element.6, f32[2,64]{1,0:T(2,128)S(1)} %get-tuple-element.5), kind=kLoop, calls=%fused_computation.2 | loop fusion | flops 512 | bytes 3584 | tf_op jit(solution)/shard_map/concatenate | solution.py:364
  1.4 38.3 %shard_map.109 = bf16[16,512]{1,0:T(8,128)(2,1)} custom-call(s32[10]{0:T(128)} %order.1, s32[2]{0:T(128)} %lens.1, bf16[16,512]{1,0:T(8,128)(2,1)} %tokens.1, f32[1,512]{1,0:T(1,128)} %bitcast.2, f32[1,512]{1,0:T(1,128)} %bitcast.3, f32[2,128]{1,0:T(2,128)} %get-tuple-element.8.cos_full, f32[2,128]{1,0:T(2,128)} %get-tuple-element.9.sin_full, ...), custom_call_target="tpu_custom_call" | custom-call | tf_op jit(solution)/shard_map/pallas_call | solution.py:372
  39.8 1.3 %copy.13 = bf16[16,512]{1,0:T(8,128)(2,1)} copy(bf16[16,512]{1,0:T(8,128)(2,1)} %shard_map.109) | data formatting | bytes 32768
  (1 shorter events, 0.0 us)

commit v2 on v1

--- a/solution.py
+++ b/solution.py
@@ -3,6 +3,7 @@
 
 import jax
 import jax.numpy as jnp
+import numpy as np
 from jax import lax
 from jax.experimental import pallas as pl
 from jax.experimental.pallas import tpu as pltpu
@@ -21,8 +22,7 @@
     tokens,
     gain1,
     gain2,
-    cos_full,
-    sin_full,
+    freq,
     wq_hbm,
     ck_hbm,
     cv_hbm,
@@ -39,8 +39,11 @@
     load_sem,
     qsend,
     qrecv,
+    nsend,
+    nrecv,
     lbuf,
     att,
+    att_send,
     heads_all,
     heads_full,
     zsend,
@@ -56,6 +59,8 @@
     down_acc,
     q_ss,
     q_rs,
+    n_ss,
+    n_rs,
     h_ss,
     h_rs,
     z_ss,
@@ -113,15 +118,19 @@
     x = tokens[...].astype(F32)
     squares = jnp.sum(x * x, axis=1, keepdims=True)
     xg = (x * gain1[...]).astype(BF16)
+    sq_lanes = jnp.broadcast_to(squares, (rows, hd))
+    for p in range(group):
+        nsend[p] = sq_lanes[p * seqs : (p + 1) * seqs]
+    angle = [lens[b].astype(F32) * freq[...] for b in range(seqs)]
+    lane = lax.broadcasted_iota(jnp.int32, (1, hd), 1)
+    cosine = [jnp.cos(a) for a in angle]
+    sine = [jnp.where(lane < hd // 2, -jnp.sin(a), jnp.sin(a)) for a in angle]
     loads[0].wait()
     for load in loads[2:]:
         load.start()
     part = jnp.dot(xg, wq[...], preferred_element_type=F32)
-    sq_lanes = jnp.broadcast_to(squares, (rows, hd))
     for p in range(group):
-        qsend[p, :, :qcols] = part[p * seqs : (p + 1) * seqs]
-        qsend[p, :, qcols:] = sq_lanes[p * seqs : (p + 1) * seqs]
-    pl.semaphore_wait(barrier, group - 1 + n_tensor - 1)
+        qsend[p] = part[p * seqs : (p + 1) * seqs].astype(BF16)
 
     def q_copy(k):
         to = lax.rem(me + k, group)
@@ -134,13 +143,30 @@
             device_id_type=MESH,
         )
 
-    for k in range(1, group):
+    def n_copy(k):
+        to = lax.rem(me + k, group)
+        return pltpu.make_async_remote_copy(
+            src_ref=nsend.at[to],
+            dst_ref=nrecv.at[k - 1],
+            send_sem=n_ss.at[k - 1],
+            recv_sem=n_rs.at[k - 1],
+            device_id=plane(to),
+            device_id_type=MESH,
+        )
+
+    pl.semaphore_wait(barrier, group - 1 + n_tensor - 1)
+    for k in range(1, group):
+        n_copy(k).start()
         q_copy(k).start()
-    total = qsend[me]
+    squares = nsend[me]
+    for k in range(1, group):
+        n_copy(k).wait_recv()
+        squares = squares + nrecv[k - 1]
+    factor = lax.rsqrt(squares / full_width + 1e-05)
+    total = qsend[me].astype(F32)
     for k in range(1, group):
         q_copy(k).wait_recv()
-        total = total + qrecv[k - 1]
-    factor = lax.rsqrt(total[:, qcols:] / full_width + 1e-05)
+        total = total + qrecv[k - 1].astype(F32)
     for g in range(groups):
         stored = [
             total[:, (g * blocks + j) * hd : (g * blocks + j + 1) * hd] * factor
@@ -159,7 +185,7 @@
     column = lax.broadcasted_iota(jnp.int32, (per_group, length), 1)
 
     def turn(vec, b):
-        return vec * cos_full[b : b + 1, :] + pltpu.roll(vec, hd // 2, 1) * sin_full[b : b + 1, :]
+        return vec * cosine[b] + pltpu.roll(vec, hd // 2, 1) * sine[b]
 
     for b in range(seqs):
         for g in range(groups):
@@ -182,7 +208,7 @@
 
     def h_copy(k):
         return pltpu.make_async_remote_copy(
-            src_ref=att,
+            src_ref=att_send,
             dst_ref=heads_all.at[me],
             send_sem=h_ss.at[k - 1],
             recv_sem=h_rs.at[k - 1],
@@ -190,14 +216,15 @@
             device_id_type=MESH,
         )
 
+    att_send[...] = att[...].astype(BF16)
     for k in range(1, group):
         h_copy(k).start()
-    heads_all[me] = att[...]
+    heads_all[me] = att_send[...]
     loads[3].wait()
     for k in range(1, group):
         h_copy(k).wait_recv()
     for p in range(group):
-        heads_full[p * seqs : (p + 1) * seqs, :] = heads_all[p]
+        heads_full[p * seqs : (p + 1) * seqs, :] = heads_all[p].astype(F32)
 
     def z_copy(stage, k):
         return pltpu.make_async_remote_copy(
@@ -317,9 +344,10 @@
         add_piece(k, act_all[k])
 
     lowered = down_acc[...].reshape(rows, width)
-    out[...] = (hidden[...].astype(F32) + tensor_sum(1, lowered)).astype(BF16)
-
-    for k in range(1, group):
+    out[...] = hidden[...].astype(F32) + tensor_sum(1, lowered)
+
+    for k in range(1, group):
+        n_copy(k).wait_send()
         q_copy(k).wait_send()
         h_copy(k).wait_send()
         s_copy(k).wait_send()
@@ -357,22 +385,18 @@
     n_heads_cols = out_weight.shape[0]
 
     half = hd // 2
-    inv_freq = 500000.0 ** (-(2.0 * jnp.arange(half, dtype=F32)) / hd)
-    angles = cache_len.astype(F32)[:, None] * inv_freq[None, :]
-    cosine = jnp.cos(angles)
-    sine = jnp.sin(angles)
-    cos_full = jnp.concatenate([cosine, cosine], axis=1)
-    sin_full = jnp.concatenate([-sine, sine], axis=1)
+    inv_freq = 500000.0 ** (-(2.0 * np.arange(half)) / hd)
+    freq = jnp.asarray(np.concatenate([inv_freq, inv_freq])[None, :], F32)
 
     vmem = pl.BlockSpec(memory_space=pltpu.VMEM)
     smem = pl.BlockSpec(memory_space=pltpu.SMEM)
     hbm = pl.BlockSpec(memory_space=pltpu.HBM)
     dma = pltpu.SemaphoreType.DMA
     peers = group - 1
-    return pl.pallas_call(
+    summed = pl.pallas_call(
         functools.partial(layer_kernel, dims),
-        out_shape=jax.ShapeDtypeStruct((rows, width), BF16),
-        in_specs=[smem, smem] + [vmem] * 5 + [hbm] * 6,
+        out_shape=jax.ShapeDtypeStruct((rows, width), F32),
+        in_specs=[smem, smem] + [vmem] * 4 + [hbm] * 6,
         out_specs=vmem,
         scratch_shapes=[
             pltpu.VMEM(qkv_weight.shape, BF16),
@@ -382,11 +406,14 @@
             pltpu.VMEM(gate_up.shape, BF16),
             pltpu.VMEM(down_weight.shape, BF16),
             dma((6,)),
-            pltpu.VMEM((group, seqs, qcols + hd), F32),
-            pltpu.VMEM((peers, seqs, qcols + hd), F32),
+            pltpu.VMEM((group, seqs, qcols), BF16),
+            pltpu.VMEM((peers, seqs, qcols), BF16),
+            pltpu.VMEM((group, seqs, hd), F32),
+            pltpu.VMEM((peers, seqs, hd), F32),
             pltpu.VMEM((seqs, groups, 16, hd), F32),
             pltpu.VMEM((seqs, n_heads_cols), F32),
-            pltpu.VMEM((group, seqs, n_heads_cols), F32),
+            pltpu.VMEM((seqs, n_heads_cols), BF16),
+            pltpu.VMEM((group, seqs, n_heads_cols), BF16),
             pltpu.VMEM((rows, n_heads_cols), F32),
             pltpu.VMEM((2, rows, width), BF16),
             pltpu.VMEM((2, n_tensor, rows, width), BF16),
@@ -399,6 +426,8 @@
             pltpu.VMEM((row_part, piece), BF16),
             pltpu.VMEM((group, row_part, piece), BF16),
             pltpu.VMEM((n_row, row_part, width), F32),
+            dma((peers,)),
+            dma((peers,)),
             dma((peers,)),
             dma((peers,)),
             dma((peers,)),
@@ -421,8 +450,7 @@
         tokens,
         attn_gain[None, :],
         ffn_gain[None, :],
-        cos_full,
-        sin_full,
+        freq,
         qkv_weight,
         cache_keys,
         cache_values,
@@ -430,6 +458,7 @@
         gate_up,
         down_weight,
     )
+    return summed.astype(BF16)
 
 
 def solution(mesh):

time: 41.3 us -> 39.4 us (0.954)
  local copies, waits for them, and re-layouts: 1.32 us -> 0 us
  Pallas kernels: 38.3 us -> 37.7 us
    unnamed x1 -> x0, local copies, waits for them, and re-layouts: 1.32 us -> none
    convert_element_type x1, other arithmetic: 0.66 us -> 1.37 us  [body(): return summed.astype(BF16)]
    concatenate x1 -> x0, other arithmetic: 0.66 us -> none  [body(): cos_full = jnp.concatenate([cosine, cosine], axis=1)]
    pallas_call x1, Pallas kernels: 38.3 us -> 37.7 us  [body(): pl.pallas_call(functools.partial(layer_kernel, dims), out_shape=jax.Shape...]
where the time goes in v2:
time: 39.4 us; the launch traced here: 39.1 us
  Pallas kernels  37.7 us (96%)
  other arithmetic  1.37 us (3%)
    pallas_call x1, Pallas kernels, body(): pl.pallas_call(functools.partial(layer_kernel, dims), out_shape=jax.Shape...  37.7 us
    convert_element_type x1, other arithmetic, body(): return summed.astype(BF16)  1.37 us

profile of v2, /device:TPU:0, one launch (start us, length us, event | category | flops | bytes accessed | tf_op | source)
XLA Modules:
  0.0 39.1 jit_solution(12007959705000296184)
XLA Ops:
  0.0 37.7 %shard_map.118 = f32[16,512]{1,0:T(8,128)} custom-call(s32[10]{0:T(128)} %order.1, s32[2]{0:T(128)} %lens.1, bf16[16,512]{1,0:T(8,128)(2,1)} %tokens.1, f32[1,512]{1,0:T(1,128)} %bitcast.2, f32[1,512]{1,0:T(1,128)} %bitcast.3, f32[1,128]{1,0:T(1,128)} %constant.2.clone.freq, bf16[512,2560]{1,0:T(8,128)(2,1)} %wq_hbm.1, bf16[2,2,4096,128]{3,2,1,0:T(8,128)(2,1)} %ck_hbm.1, ...), custom_call_target="tpu_custom_call" | custom-call | tf_op jit(solution)/shard_map/pallas_call | solution.py:396
  37.8 1.4 %convert_element_type.3 = bf16[16,512]{1,0:T(8,128)(2,1)} convert(f32[16,512]{1,0:T(8,128)} %shard_map.118) | non-fusion elementwise | flops 8192 | bytes 49152 | tf_op jit(solution)/shard_map/convert_element_type | solution.py:461
